TPU v7x, 32 devices: a whole 2x2x4 slice. The times are simulated.
32 devices in a mesh: section: 2 (over core), fsdp: 4 (over y, x), tp: 4 (over z).
Axes of the slice: x: 2, y: 2, z: 4, core: 2. Of those that a mesh axis runs over, the one named last changes fastest.
Arguments:
- saved_inputs: bfloat16 [2, 8, 256, 2560], P('section', None, 'fsdp', 'tp'), may hold values from -6 to 6
- top_grad: bfloat16 [8, 256, 2560], P(None, 'fsdp', 'tp'), may hold values from -6 to 6
- norm_gain: float32 [2, 2560], P('section'), may hold values from 0.5 to 1.5
- gate_weight: bfloat16 [2, 2560, 6912], P('section', 'fsdp', 'tp'), may hold values from -0.125 to 0.125
- up_weight: bfloat16 [2, 2560, 6912], P('section', 'fsdp', 'tp'), may hold values from -0.125 to 0.125
- down_weight: bfloat16 [2, 6912, 2560], P('section', 'tp', 'fsdp'), may hold values from -0.078125 to 0.078125
Outputs:
- input_grads: bfloat16 [2, 8, 256, 2560], P('section', None, 'fsdp', 'tp')
- gate_grad: float32 [2, 2560, 6912], P('section', 'fsdp', 'tp')
- up_grad: float32 [2, 2560, 6912], P('section', 'fsdp', 'tp')
- down_grad: float32 [2, 6912, 2560], P('section', 'tp', 'fsdp')
- gain_grad: float32 [2, 2560], P('section', 'tp')
All inputs are finite; a program needn't handle non-finite values.
Results may differ from a plain program's by a relative error of at most 0.0055.
Values may be sent and summed in bfloat16 or wider, within the bound.
A program may use at most 192 MiB of HBM per device.

v0:
```python
import jax
import jax.numpy as jnp
from jax import lax
from jax.sharding import PartitionSpec as P

epsilon = 1e-05


def for_sending(x):

    def short(part):
        return part.astype(jnp.bfloat16) if part.dtype == jnp.float32 else part

    return jax.tree.map(short, x)


def passed_along(block, axis, distance):
    devices = range(lax.axis_size(axis))
    route = [(i - distance, i) for i in devices if i - distance in devices]
    return lax.ppermute(block, axis, route)


def select_micro(buffer, micro_index):
    return lax.dynamic_index_in_dim(buffer, micro_index, 0, keepdims=False)


def store_micro(buffer, micro_index, update, condition):
    previous = select_micro(buffer, micro_index)
    return lax.dynamic_update_index_in_dim(
        buffer, jnp.where(condition, update, previous), micro_index, 0
    )


def contract_rows(left, right):
    return lax.dot_general(
        left, right, (((0,), (0,)), ((), ())), preferred_element_type=jnp.float32
    )


def contract_cols(left, right):
    return lax.dot_general(
        left, right, (((1,), (1,)), ((), ())), preferred_element_type=jnp.float32
    )


def shards(saved_inputs, top_grad, norm_gain, gate_weight, up_weight, down_weight):
    section_count = lax.axis_size("section")
    section_index = lax.axis_index("section")
    tp_count = lax.axis_size("tp")
    micro_count = saved_inputs.shape[1]
    row_count = saved_inputs.shape[2]
    local_width = saved_inputs.shape[3]
    full_width = local_width * tp_count
    w_gate, w_up, w_down = (
        lax.all_gather(gate_weight[0], "fsdp", axis=0, tiled=True),
        lax.all_gather(up_weight[0], "fsdp", axis=0, tiled=True),
        lax.all_gather(down_weight[0], "fsdp", axis=1, tiled=True),
    )
    hidden_width = w_gate.shape[1]
    gain_full = norm_gain[0]
    column_start = lax.axis_index("tp") * local_width
    gain_local = lax.dynamic_slice_in_dim(gain_full, column_start, local_width)
    inputs_local = saved_inputs[0]
    inputs_full = lax.all_gather(inputs_local, "tp", axis=2, tiled=True)
    inputs_wide = inputs_full.astype(jnp.float32)
    row_scale = lax.rsqrt(jnp.mean(inputs_wide * inputs_wide, axis=-1, keepdims=True) + epsilon)
    normed = (inputs_wide * row_scale * gain_full).astype(jnp.bfloat16)
    gate_pre = jnp.einsum("mtd,df->mtf", normed, w_gate, preferred_element_type=jnp.float32)
    upward = jnp.einsum("mtd,df->mtf", normed, w_up, preferred_element_type=jnp.float32)
    gate_sigmoid = jax.nn.sigmoid(gate_pre)
    silu_out = gate_pre * gate_sigmoid
    hidden = (silu_out * upward).astype(jnp.bfloat16)
    last_section = section_index == section_count - 1

    def one_tick(tick_number, loop_state):
        received, grads_out, gain_total, stored = loop_state
        micro_raw = tick_number - (section_count - 1 - section_index)
        is_valid = (micro_raw >= 0) & (micro_raw < micro_count)
        micro_index = jnp.clip(micro_raw, 0, micro_count - 1)
        top_piece = select_micro(top_grad, micro_index)
        cotangent = jnp.where(last_section, top_piece, received)
        full_cotangent = lax.all_gather(for_sending(cotangent), "tp", axis=1, tiled=True).astype(
            cotangent.dtype
        )
        gate_now = select_micro(gate_pre, micro_index)
        upward_now = select_micro(upward, micro_index)
        sigmoid_now = select_micro(gate_sigmoid, micro_index)
        silu_now = select_micro(silu_out, micro_index)
        d_hidden = contract_cols(full_cotangent, w_down)
        d_gate = (
            d_hidden * upward_now * sigmoid_now * (1.0 + gate_now * (1.0 - sigmoid_now))
        ).astype(jnp.bfloat16)
        d_up = (d_hidden * silu_now).astype(jnp.bfloat16)
        partial_value = contract_cols(d_gate, w_gate) + contract_cols(d_up, w_up)
        scale_now = select_micro(row_scale, micro_index)
        unit_local = select_micro(inputs_local, micro_index).astype(jnp.float32) * scale_now
        unit_full = select_micro(inputs_wide, micro_index) * scale_now
        d_normed_full = lax.psum(partial_value, "tp")
        norm_stat = jnp.mean(d_normed_full * gain_full * unit_full, axis=-1, keepdims=True)
        d_normed = lax.dynamic_slice_in_dim(d_normed_full, column_start, local_width, 1)
        scaled = d_normed * gain_local
        d_inputs = (
            cotangent.astype(jnp.float32) + scale_now * (scaled - unit_local * norm_stat)
        ).astype(jnp.bfloat16)
        grads_out = store_micro(grads_out, micro_index, d_inputs, is_valid)
        valid_float = is_valid.astype(jnp.float32)
        gain_total = gain_total + valid_float * jnp.sum(d_normed * unit_local, axis=0)
        valid_weight = is_valid.astype(jnp.bfloat16)
        normed_now = select_micro(normed, micro_index)
        hidden_now = select_micro(hidden, micro_index)
        stored = (
            stored[0] + contract_rows(normed_now, d_gate * valid_weight),
            stored[1] + contract_rows(normed_now, d_up * valid_weight),
            stored[2] + contract_rows(full_cotangent * valid_weight, hidden_now),
        )
        handed = passed_along(d_inputs, "section", -1)
        return (handed, grads_out, gain_total, stored)

    stored_init = (
        jnp.zeros((full_width, hidden_width), jnp.float32),
        jnp.zeros((full_width, hidden_width), jnp.float32),
        jnp.zeros((full_width, hidden_width), jnp.float32),
    )
    initial = (
        jnp.zeros((row_count, local_width), jnp.bfloat16),
        jnp.zeros((micro_count, row_count, local_width), jnp.bfloat16),
        jnp.zeros((local_width,), jnp.float32),
        stored_init,
    )
    handed_last, grads_out, gain_total, stored = lax.fori_loop(
        0, micro_count + section_count - 1, one_tick, initial
    )
    gate_share, up_share, down_share = (
        lax.psum_scatter(stored[0], "fsdp", scatter_dimension=0, tiled=True),
        lax.psum_scatter(stored[1], "fsdp", scatter_dimension=0, tiled=True),
        lax.psum_scatter(stored[2], "fsdp", scatter_dimension=0, tiled=True),
    )
    gain_share = lax.psum(gain_total, "fsdp")
    return (grads_out[None], gate_share[None], up_share[None], down_share.T[None], gain_share[None])


def solution(mesh):
    placed = (
        P("section", None, "fsdp", "tp"),
        P(None, "fsdp", "tp"),
        P("section", None),
        P("section", "fsdp", "tp"),
        P("section", "fsdp", "tp"),
        P("section", "tp", "fsdp"),
    )
    return jax.shard_map(
        shards,
        mesh=mesh,
        in_specs=placed,
        out_specs=(
            P("section", None, "fsdp", "tp"),
            P("section", "fsdp", "tp"),
            P("section", "fsdp", "tp"),
            P("section", "tp", "fsdp"),
            P("section", "tp"),
        ),
        check_vma=False,
    )
```

profile of v0, /device:TPU:0, one launch (start us, length us, event | category | flops | bytes accessed | tf_op | source)
XLA Modules:
  0.0 1582.6 jit_solution(9711850092869869036)
XLA Ops:
  10.1 56.8 %all-gather.9.cloned.1.call-done = bf16[1,8,64,2560]{3,2,1,0:T(8,128)(2,1)} async-done(((bf16[1,8,64,640]{3,2,1,0:T(8,128)(2,1)}), bf16[1,8,64,2560]{3,2,1,0:T(8,128)(2,1)}) %all-gather.9.cloned.1.call-update) | async-done | bytes 2621456 | tf_op jit(solution)/shard_map/all_gather | solution.py:64
  75.1 83.7 %all-gather.13.cloned.1.call-done = bf16[1,2560,1728]{1,2,0:T(8,128)(2,1)} async-done(((bf16[1,640,1728]{1,2,0:T(8,128)(2,1)}), bf16[1,2560,1728]{1,2,0:T(8,128)(2,1)}) %all-gather.13.cloned.1.call-update) | async-done | bytes 8847376 | tf_op jit(solution)/shard_map/all_gather | solution.py:56
  158.8 13.1 copy.12
  171.8 80.1 %all-gather.15.cloned.1.call-done = bf16[1,2560,1728]{1,2,0:T(8,128)(2,1)} async-done(((bf16[1,640,1728]{1,2,0:T(8,128)(2,1)}), bf16[1,2560,1728]{1,2,0:T(8,128)(2,1)}) %all-gather.15.cloned.1.call-update) | async-done | bytes 8847376 | tf_op jit(solution)/shard_map/all_gather | solution.py:55
  251.9 13.1 copy.11
  265.0 7.5 fusion.29
  274.4 11.5 multiply_convert_fusion.1
  285.9 59.1 %all-gather.11.cloned.1.call-done = bf16[1,1728,2560]{2,1,0:T(8,128)(2,1)} async-done(((bf16[1,1728,640]{2,1,0:T(8,128)(2,1)}), bf16[1,1728,2560]{2,1,0:T(8,128)(2,1)}) %all-gather.11.cloned.1.call-update) | async-done | bytes 8847376 | tf_op jit(solution)/shard_map/all_gather | solution.py:57
  345.9 734.4 %while.26 = (s32[]{:T(128)}, bf16[64,640]{1,0:T(8,128)(2,1)S(1)}, bf16[8,64,640]{2,1,0:T(8,128)(2,1)}, f32[640]{0:T(1024)S(1)}, f32[2560,1728]{0,1:T(8,128)}, /*...) while((s32[]{:T(128)}, bf16[64,640]{1,0:T(8,128)(2,1)S(1)}, ...), condition=%wide.region_5.6_spmd.clone, body=%wide.region_1.5_spmd.clone.sunk | while | flops 3426907392 | bytes 217691936 | solution.py:130
  346.8 14.2 all_gather.27
  361.0 6.8 fusion.73
  376.7 9.6 select_add_fusion.11
  386.3 8.5 select_add_fusion.10
  394.8 8.6 select_add_fusion.9
  403.4 13.2 all-reduce.2.cloned.1.call-done
  423.9 14.4 all_gather.27
  438.3 6.8 fusion.73
  454.1 14.9 select_add_fusion.11
  469.0 14.6 select_add_fusion.10
  483.6 14.7 select_add_fusion.9
  505.7 14.4 all_gather.27
  520.1 6.8 fusion.73
  530.5 3.7 convolution_add_fusion.2
  535.8 14.9 select_add_fusion.11
  550.7 14.6 select_add_fusion.10
  565.4 14.7 select_add_fusion.9
  587.4 14.4 all_gather.27
  601.8 6.8 fusion.73
  612.3 3.7 convolution_add_fusion.2
  617.6 14.9 select_add_fusion.11
  632.5 14.7 select_add_fusion.10
  647.2 14.7 select_add_fusion.9
  669.2 14.7 all_gather.27
  683.9 6.8 fusion.73
  694.3 3.7 convolution_add_fusion.2
  699.6 14.9 select_add_fusion.11
  714.5 14.7 select_add_fusion.10
  729.2 14.7 select_add_fusion.9
  751.3 15.1 all_gather.27
  766.3 6.8 fusion.73
  776.8 3.7 convolution_add_fusion.2
  782.1 14.9 select_add_fusion.11
  797.0 14.7 select_add_fusion.10
  811.7 14.7 select_add_fusion.9
  833.7 15.1 all_gather.27
  848.8 6.8 fusion.73
  864.6 14.9 select_add_fusion.11
  879.5 14.7 select_add_fusion.10
  894.2 14.7 select_add_fusion.9
  916.2 15.1 all_gather.27
  931.3 6.8 fusion.73
  947.0 14.9 select_add_fusion.11
  962.0 14.7 select_add_fusion.10
  976.6 14.7 select_add_fusion.9
  998.7 15.1 all_gather.27
  1013.8 6.8 fusion.73
  1024.2 3.7 convolution_add_fusion.2
  1029.5 14.9 select_add_fusion.11
  1044.4 14.7 select_add_fusion.10
  1059.1 14.7 select_add_fusion.9
  1082.0 9.5 psum.20
  1091.5 155.1 %reduce-scatter.6.cloned.1.call-done = f32[640,1728]{0,1:T(8,128)} async-done(((f32[2560,1728]{0,1:T(8,128)}), f32[640,1728]{0,1:T(8,128)}) %reduce-scatter.6.cloned.1.call-update) | async-done | bytes 4423696 | tf_op jit(solution)/shard_map/reduce_scatter | solution.py:135
  1246.5 164.8 %reduce-scatter.8.cloned.1.call-done = f32[640,1728]{0,1:T(8,128)} async-done(((f32[2560,1728]{0,1:T(8,128)}), f32[640,1728]{0,1:T(8,128)}) %reduce-scatter.8.cloned.1.call-update) | async-done | bytes 4423696 | tf_op jit(solution)/shard_map/reduce_scatter | solution.py:136
  1411.3 164.8 %reduce-scatter.4.cloned.1.call-done = f32[640,1728]{0,1:T(8,128)} async-done(((f32[2560,1728]{0,1:T(8,128)}), f32[640,1728]{0,1:T(8,128)}) %reduce-scatter.4.cloned.1.call-update) | async-done | bytes 4423696 | tf_op jit(solution)/shard_map/reduce_scatter | solution.py:134
  (225 shorter events, 142.4 us)
Async XLA Ops:
  7.2 2.9 copy-start.5
  7.2 59.7 %all-gather.9.cloned.1.call-start = ((), (), s32[]{:S(2)}) async-start(), calls=%async_computation.6 | async-start | bytes 3276800 | tf_op jit(solution)/shard_map/all_gather | solution.py:64
  7.9 150.8 %all-gather.13.cloned.1.call-start = ((), (), s32[]{:S(2)}) async-start(), calls=%async_computation.8 | async-start | bytes 11059200 | tf_op jit(solution)/shard_map/all_gather | solution.py:56
  8.7 243.3 %all-gather.15.cloned.1.call-start = ((), (), s32[]{:S(2)}) async-start(), calls=%async_computation.9 | async-start | bytes 11059200 | tf_op jit(solution)/shard_map/all_gather | solution.py:55
  9.4 335.6 %all-gather.11.cloned.1.call-start = ((), (), s32[]{:S(2)}) async-start(), calls=%async_computation.7 | async-start | bytes 11059200 | tf_op jit(solution)/shard_map/all_gather | solution.py:57
  66.9 4.9 copy-start.2
  272.6 1.8 copy-start.4
  345.9 70.7 %all-reduce.2.cloned.1.call-start = ((), (), s32[]{:S(2)}) async-start(), calls=%async_computation.10 | async-start | bytes 1310720 | tf_op jit(solution)/shard_map/while/body/eval_jaxpr/psum | solution.py:98
  361.0 6.9 copy-start
  367.8 3.6 copy-start.1
  394.8 23.3 %copy-start.3 = (bf16[1,64,640]{2,1,0:T(8,128)(2,1)S(1)}, bf16[1,64,640]{2,1,0:T(8,128)(2,1)}, u32[]{:S(2)}) copy-start(bf16[1,64,640]{2,1,0:T(8,128)(2,1)} %constant_dynamic-slice_fusion.3) | copy-start | bytes 245764 | tf_op jit(solution)/shard_map/while
  419.9 3.2 collective-permute-start
  423.0 75.3 %all-reduce.2.cloned.1.call-start = ((), (), s32[]{:S(2)}) async-start(), calls=%async_computation.10 | async-start | bytes 1310720 | tf_op jit(solution)/shard_map/while/body/eval_jaxpr/psum | solution.py:98
  438.3 6.9 copy-start
  445.2 3.6 copy-start.1
  483.6 16.2 %copy-start.3 = (bf16[1,64,640]{2,1,0:T(8,128)(2,1)S(1)}, bf16[1,64,640]{2,1,0:T(8,128)(2,1)}, u32[]{:S(2)}) copy-start(bf16[1,64,640]{2,1,0:T(8,128)(2,1)} %constant_dynamic-slice_fusion.3) | copy-start | bytes 245764 | tf_op jit(solution)/shard_map/while
  501.6 3.2 collective-permute-start
  504.8 75.3 %all-reduce.2.cloned.1.call-start = ((), (), s32[]{:S(2)}) async-start(), calls=%async_computation.10 | async-start | bytes 1310720 | tf_op jit(solution)/shard_map/while/body/eval_jaxpr/psum | solution.py:98
  520.1 6.8 copy-start
  526.9 3.6 copy-start.1
  565.4 16.2 %copy-start.3 = (bf16[1,64,640]{2,1,0:T(8,128)(2,1)S(1)}, bf16[1,64,640]{2,1,0:T(8,128)(2,1)}, u32[]{:S(2)}) copy-start(bf16[1,64,640]{2,1,0:T(8,128)(2,1)} %constant_dynamic-slice_fusion.3) | copy-start | bytes 245764 | tf_op jit(solution)/shard_map/while
  583.4 3.2 collective-permute-start
  586.5 75.3 %all-reduce.2.cloned.1.call-start = ((), (), s32[]{:S(2)}) async-start(), calls=%async_computation.10 | async-start | bytes 1310720 | tf_op jit(solution)/shard_map/while/body/eval_jaxpr/psum | solution.py:98
  601.8 6.8 copy-start
  608.6 3.6 copy-start.1
  647.2 16.2 %copy-start.3 = (bf16[1,64,640]{2,1,0:T(8,128)(2,1)S(1)}, bf16[1,64,640]{2,1,0:T(8,128)(2,1)}, u32[]{:S(2)}) copy-start(bf16[1,64,640]{2,1,0:T(8,128)(2,1)} %constant_dynamic-slice_fusion.3) | copy-start | bytes 245764 | tf_op jit(solution)/shard_map/while
  665.1 3.2 collective-permute-start
  668.3 75.6 %all-reduce.2.cloned.1.call-start = ((), (), s32[]{:S(2)}) async-start(), calls=%async_computation.10 | async-start | bytes 1310720 | tf_op jit(solution)/shard_map/while/body/eval_jaxpr/psum | solution.py:98
  683.9 6.8 copy-start
  690.7 3.6 copy-start.1
  729.2 16.2 %copy-start.3 = (bf16[1,64,640]{2,1,0:T(8,128)(2,1)S(1)}, bf16[1,64,640]{2,1,0:T(8,128)(2,1)}, u32[]{:S(2)}) copy-start(bf16[1,64,640]{2,1,0:T(8,128)(2,1)} %constant_dynamic-slice_fusion.3) | copy-start | bytes 245764 | tf_op jit(solution)/shard_map/while
  747.2 3.2 collective-permute-start
  750.3 76.0 %all-reduce.2.cloned.1.call-start = ((), (), s32[]{:S(2)}) async-start(), calls=%async_computation.10 | async-start | bytes 1310720 | tf_op jit(solution)/shard_map/while/body/eval_jaxpr/psum | solution.py:98
  766.3 6.8 copy-start
  773.2 3.6 copy-start.1
  811.7 16.2 %copy-start.3 = (bf16[1,64,640]{2,1,0:T(8,128)(2,1)S(1)}, bf16[1,64,640]{2,1,0:T(8,128)(2,1)}, u32[]{:S(2)}) copy-start(bf16[1,64,640]{2,1,0:T(8,128)(2,1)} %constant_dynamic-slice_fusion.3) | copy-start | bytes 245764 | tf_op jit(solution)/shard_map/while
  829.7 3.2 collective-permute-start
  832.8 76.0 %all-reduce.2.cloned.1.call-start = ((), (), s32[]{:S(2)}) async-start(), calls=%async_computation.10 | async-start | bytes 1310720 | tf_op jit(solution)/shard_map/while/body/eval_jaxpr/psum | solution.py:98
  848.8 6.8 copy-start
  855.6 3.6 copy-start.1
  894.2 16.2 %copy-start.3 = (bf16[1,64,640]{2,1,0:T(8,128)(2,1)S(1)}, bf16[1,64,640]{2,1,0:T(8,128)(2,1)}, u32[]{:S(2)}) copy-start(bf16[1,64,640]{2,1,0:T(8,128)(2,1)} %constant_dynamic-slice_fusion.3) | copy-start | bytes 245764 | tf_op jit(solution)/shard_map/while
  912.1 3.2 collective-permute-start
  915.3 76.0 %all-reduce.2.cloned.1.call-start = ((), (), s32[]{:S(2)}) async-start(), calls=%async_computation.10 | async-start | bytes 1310720 | tf_op jit(solution)/shard_map/while/body/eval_jaxpr/psum | solution.py:98
  931.3 6.8 copy-start
  938.1 3.6 copy-start.1
  976.6 16.2 %copy-start.3 = (bf16[1,64,640]{2,1,0:T(8,128)(2,1)S(1)}, bf16[1,64,640]{2,1,0:T(8,128)(2,1)}, u32[]{:S(2)}) copy-start(bf16[1,64,640]{2,1,0:T(8,128)(2,1)} %constant_dynamic-slice_fusion.3) | copy-start | bytes 245764 | tf_op jit(solution)/shard_map/while
  994.6 3.2 collective-permute-start
  997.8 76.0 %all-reduce.2.cloned.1.call-start = ((), (), s32[]{:S(2)}) async-start(), calls=%async_computation.10 | async-start | bytes 1310720 | tf_op jit(solution)/shard_map/while/body/eval_jaxpr/psum | solution.py:98
  1013.8 6.8 copy-start
  1020.6 3.6 copy-start.1
  1059.1 16.2 %copy-start.3 = (bf16[1,64,640]{2,1,0:T(8,128)(2,1)S(1)}, bf16[1,64,640]{2,1,0:T(8,128)(2,1)}, u32[]{:S(2)}) copy-start(bf16[1,64,640]{2,1,0:T(8,128)(2,1)} %constant_dynamic-slice_fusion.3) | copy-start | bytes 245764 | tf_op jit(solution)/shard_map/while
  1077.1 3.2 collective-permute-start
  1080.2 166.3 %reduce-scatter.6.cloned.1.call-start = ((), (), s32[]{:S(2)}) async-start(), calls=%async_computation.4 | async-start | bytes 22118400 | tf_op jit(solution)/shard_map/reduce_scatter | solution.py:135
  1080.8 330.5 %reduce-scatter.8.cloned.1.call-start = ((), (), s32[]{:S(2)}) async-start(), calls=%async_computation.5 | async-start | bytes 22118400 | tf_op jit(solution)/shard_map/reduce_scatter | solution.py:136
  1081.4 494.7 %reduce-scatter.4.cloned.1.call-start = ((), (), s32[]{:S(2)}) async-start(), calls=%async_computation.3 | async-start | bytes 22118400 | tf_op jit(solution)/shard_map/reduce_scatter | solution.py:134
Sparse Core Ops, SparseCore 0:
  9.6 57.2 all-gather.8
  68.7 89.9 all-gather.12
  160.6 91.2 all-gather.14
  253.6 91.2 all-gather.10
  375.3 41.2 all-reduce.1
  452.6 40.0 all-reduce.1
  534.3 40.3 all-reduce.1
  616.1 40.8 all-reduce.1
  698.1 41.2 all-reduce.1
  780.6 41.2 all-reduce.1
  863.1 41.1 all-reduce.1
  945.6 41.1 all-reduce.1
  1028.0 41.1 all-reduce.1
  1084.4 162.0 reduce-scatter.5
  1250.1 161.1 reduce-scatter.7
  1414.9 161.1 reduce-scatter.3
where the time goes:
time: 1590 us; the launch traced here: 1580 us
  waiting for transfers between devices  789 us (50%)
  matrix products  520 us (33%)
  blocking collectives  142 us (9%)
  other arithmetic  55.5 us (3%)
  local copies, waits for them, and re-layouts  49.3 us (3%)
    dot_general x27, matrix products, contract_rows(): lax.dot_general(left, right, (((0,), (0,)), ((), ())), preferred_element_...  381 us
    reduce_scatter x1, waiting for transfers between devices, shards(): lax.psum_scatter(stored[0], 'fsdp', scatter_dimension=0, tiled=True)  165 us
    reduce_scatter x1, waiting for transfers between devices, shards(): lax.psum_scatter(stored[2], 'fsdp', scatter_dimension=0, tiled=True)  165 us
    reduce_scatter x1, waiting for transfers between devices, shards(): lax.psum_scatter(stored[1], 'fsdp', scatter_dimension=0, tiled=True)  155 us
    all_gather x9, blocking collectives, one_tick(): lax.all_gather(for_sending(cotangent), 'tp', axis=1, tiled=True)  132 us
    dot_general x27, matrix products, contract_cols(): lax.dot_general(left, right, (((1,), (1,)), ((), ())), preferred_element_...  121 us
    all_gather x1, waiting for transfers between devices, shards(): lax.all_gather(up_weight[0], 'fsdp', axis=0, tiled=True)  83.7 us
    all_gather x1, waiting for transfers between devices, shards(): lax.all_gather(gate_weight[0], 'fsdp', axis=0, tiled=True)  80.1 us
  transfers between devices with their start and end apart: 25, of which 17 were waited for; matrix products, arithmetic and copies ran while one was open for 29% of the time, Pallas kernels for 0%

commit v1 on v0

--- a/solution.py
+++ b/solution.py
@@ -79,9 +79,9 @@
         micro_index = jnp.clip(micro_raw, 0, micro_count - 1)
         top_piece = select_micro(top_grad, micro_index)
         cotangent = jnp.where(last_section, top_piece, received)
-        full_cotangent = lax.all_gather(for_sending(cotangent), "tp", axis=1, tiled=True).astype(
-            cotangent.dtype
-        )
+        full_cotangent = jnp.concatenate(
+            lax.all_gather(for_sending(cotangent), "tp"), axis=1
+        ).astype(cotangent.dtype)
         gate_now = select_micro(gate_pre, micro_index)
         upward_now = select_micro(upward, micro_index)
         sigmoid_now = select_micro(gate_sigmoid, micro_index)

time: 1590 us -> 1590 us (level)
  no operation moved by 1% of the time
where the time goes in v1:
time: 1590 us
  waiting for transfers between devices  788 us (50%)
  matrix products  520 us (33%)
  blocking collectives  141 us (9%)
  other arithmetic  57.9 us (4%)
  local copies, waits for them, and re-layouts  52.2 us (3%)
    dot_general x27, matrix products, contract_rows(): lax.dot_general(left, right, (((0,), (0,)), ((), ())), preferred_element_...  381 us
    reduce_scatter x1, waiting for transfers between devices, shards(): lax.psum_scatter(stored[0], 'fsdp', scatter_dimension=0, tiled=True)  165 us
    reduce_scatter x1, waiting for transfers between devices, shards(): lax.psum_scatter(stored[2], 'fsdp', scatter_dimension=0, tiled=True)  165 us
    reduce_scatter x1, waiting for transfers between devices, shards(): lax.psum_scatter(stored[1], 'fsdp', scatter_dimension=0, tiled=True)  155 us
    all_gather x9, blocking collectives, one_tick(): lax.all_gather(for_sending(cotangent), 'tp')  132 us
    dot_general x27, matrix products, contract_cols(): lax.dot_general(left, right, (((1,), (1,)), ((), ())), preferred_element_...  121 us
    all_gather x1, waiting for transfers between devices, shards(): lax.all_gather(up_weight[0], 'fsdp', axis=0, tiled=True)  83.7 us
    all_gather x1, waiting for transfers between devices, shards(): lax.all_gather(gate_weight[0], 'fsdp', axis=0, tiled=True)  80.1 us
  transfers between devices with their start and end apart: 25, of which 17 were waited for; matrix products, arithmetic and copies ran while one was open for 29% of the time, Pallas kernels for 0%

profile of v1, /device:TPU:0, one launch (start us, length us, event | category | flops | bytes accessed | tf_op | source)
XLA Modules:
  0.0 1587.2 jit_solution(5817512145805291112)
XLA Ops:
  10.1 56.8 %all-gather.13.cloned.1.call-done = bf16[1,8,64,2560]{3,2,1,0:T(8,128)(2,1)} async-done(((bf16[1,8,64,640]{3,2,1,0:T(8,128)(2,1)}), bf16[1,8,64,2560]{3,2,1,0:T(8,128)(2,1)}) %all-gather.13.cloned.1.call-update) | async-done | bytes 2621456 | tf_op jit(solution)/shard_map/all_gather | solution.py:64
  75.1 83.7 %all-gather.17.cloned.1.call-done = bf16[1,2560,1728]{1,2,0:T(8,128)(2,1)} async-done(((bf16[1,640,1728]{1,2,0:T(8,128)(2,1)}), bf16[1,2560,1728]{1,2,0:T(8,128)(2,1)}) %all-gather.17.cloned.1.call-update) | async-done | bytes 8847376 | tf_op jit(solution)/shard_map/all_gather | solution.py:56
  158.8 13.1 copy.15
  171.8 80.1 %all-gather.19.cloned.1.call-done = bf16[1,2560,1728]{1,2,0:T(8,128)(2,1)} async-done(((bf16[1,640,1728]{1,2,0:T(8,128)(2,1)}), bf16[1,2560,1728]{1,2,0:T(8,128)(2,1)}) %all-gather.19.cloned.1.call-update) | async-done | bytes 8847376 | tf_op jit(solution)/shard_map/all_gather | solution.py:55
  251.9 13.1 copy.14
  265.0 7.5 fusion.27
  274.4 11.5 multiply_convert_fusion.1
  285.9 59.1 %all-gather.15.cloned.1.call-done = bf16[1,1728,2560]{2,1,0:T(8,128)(2,1)} async-done(((bf16[1,1728,640]{2,1,0:T(8,128)(2,1)}), bf16[1,1728,2560]{2,1,0:T(8,128)(2,1)}) %all-gather.15.cloned.1.call-update) | async-done | bytes 8847376 | tf_op jit(solution)/shard_map/all_gather | solution.py:57
  345.9 738.7 %while.26 = (s32[]{:T(128)}, bf16[64,640]{1,0:T(8,128)(2,1)S(1)}, bf16[8,64,640]{2,1,0:T(8,128)(2,1)}, f32[640]{0:T(1024)S(1)}, f32[2560,1728]{0,1:T(8,128)}, /*...) while((s32[]{:T(128)}, bf16[64,640]{1,0:T(8,128)(2,1)S(1)}, ...), condition=%wide.region_5.6_spmd.clone, body=%wide.region_1.5_spmd.clone.sunk | while | flops 3426907392 | bytes 220313376 | solution.py:130
  346.8 14.2 all-gather.7
  361.3 6.8 fusion.72
  377.4 8.5 select_add_fusion.10
  385.9 9.6 select_add_fusion.11
  395.4 8.6 select_add_fusion.9
  404.0 12.9 all-reduce.2.cloned.1.call-done
  424.2 14.4 all-gather.7
  439.0 6.8 fusion.72
  449.5 3.7 convolution_add_fusion.2
  455.1 14.7 select_add_fusion.10
  469.8 14.9 select_add_fusion.11
  484.6 14.7 select_add_fusion.9
  506.7 14.3 all-gather.7
  521.3 6.8 fusion.72
  531.8 3.7 convolution_add_fusion.2
  537.4 14.7 select_add_fusion.10
  552.1 14.9 select_add_fusion.11
  566.9 14.7 select_add_fusion.9
  589.0 14.3 all-gather.7
  603.6 6.8 fusion.72
  614.1 3.7 convolution_add_fusion.2
  619.7 14.7 select_add_fusion.10
  634.4 14.9 select_add_fusion.11
  649.3 14.7 select_add_fusion.9
  671.3 14.3 all-gather.7
  686.0 6.8 fusion.72
  702.0 14.7 select_add_fusion.10
  716.7 14.9 select_add_fusion.11
  731.6 14.7 select_add_fusion.9
  753.6 14.8 all-gather.7
  768.7 6.8 fusion.72
  779.2 3.7 convolution_add_fusion.2
  784.8 14.7 select_add_fusion.10
  799.5 14.9 select_add_fusion.11
  814.3 14.7 select_add_fusion.9
  836.4 15.1 all-gather.7
  851.7 6.8 fusion.72
  867.8 14.7 select_add_fusion.10
  882.5 14.9 select_add_fusion.11
  897.4 14.7 select_add_fusion.9
  919.4 15.1 all-gather.7
  934.8 6.8 fusion.72
  950.9 14.7 select_add_fusion.10
  965.5 14.9 select_add_fusion.11
  980.4 14.7 select_add_fusion.9
  1002.5 15.1 all-gather.7
  1017.8 6.8 fusion.72
  1028.3 3.7 convolution_add_fusion.2
  1033.9 14.7 select_add_fusion.10
  1048.6 14.9 select_add_fusion.11
  1063.5 14.7 select_add_fusion.9
  1086.3 9.8 psum.20
  1096.2 155.0 %reduce-scatter.6.cloned.1.call-done = f32[640,1728]{0,1:T(8,128)} async-done(((f32[2560,1728]{0,1:T(8,128)}), f32[640,1728]{0,1:T(8,128)}) %reduce-scatter.6.cloned.1.call-update) | async-done | bytes 4423696 | tf_op jit(solution)/shard_map/reduce_scatter | solution.py:135
  1251.1 164.8 %reduce-scatter.8.cloned.1.call-done = f32[640,1728]{0,1:T(8,128)} async-done(((f32[2560,1728]{0,1:T(8,128)}), f32[640,1728]{0,1:T(8,128)}) %reduce-scatter.8.cloned.1.call-update) | async-done | bytes 4423696 | tf_op jit(solution)/shard_map/reduce_scatter | solution.py:136
  1415.9 164.8 %reduce-scatter.4.cloned.1.call-done = f32[640,1728]{0,1:T(8,128)} async-done(((f32[2560,1728]{0,1:T(8,128)}), f32[640,1728]{0,1:T(8,128)}) %reduce-scatter.4.cloned.1.call-update) | async-done | bytes 4423696 | tf_op jit(solution)/shard_map/reduce_scatter | solution.py:134
  (261 shorter events, 147.7 us)
Async XLA Ops:
  7.2 2.9 copy-start.5
  7.2 59.7 %all-gather.13.cloned.1.call-start = ((), (), s32[]{:S(2)}) async-start(), calls=%async_computation.6 | async-start | bytes 3276800 | tf_op jit(solution)/shard_map/all_gather | solution.py:64
  7.9 150.8 %all-gather.17.cloned.1.call-start = ((), (), s32[]{:S(2)}) async-start(), calls=%async_computation.8 | async-start | bytes 11059200 | tf_op jit(solution)/shard_map/all_gather | solution.py:56
  8.7 243.3 %all-gather.19.cloned.1.call-start = ((), (), s32[]{:S(2)}) async-start(), calls=%async_computation.9 | async-start | bytes 11059200 | tf_op jit(solution)/shard_map/all_gather | solution.py:55
  9.4 335.6 %all-gather.15.cloned.1.call-start = ((), (), s32[]{:S(2)}) async-start(), calls=%async_computation.7 | async-start | bytes 11059200 | tf_op jit(solution)/shard_map/all_gather | solution.py:57
  66.9 4.9 copy-start.2
  272.6 1.8 copy-start.4
  345.9 71.0 %all-reduce.2.cloned.1.call-start = ((), (), s32[]{:S(2)}) async-start(), calls=%async_computation.10 | async-start | bytes 1310720 | tf_op jit(solution)/shard_map/while/body/eval_jaxpr/psum | solution.py:98
  361.3 6.9 copy-start
  368.1 3.6 copy-start.1
  395.4 23.0 %copy-start.3 = (bf16[1,64,640]{2,1,0:T(8,128)(2,1)S(1)}, bf16[1,64,640]{2,1,0:T(8,128)(2,1)}, u32[]{:S(2)}) copy-start(bf16[1,64,640]{2,1,0:T(8,128)(2,1)} %constant_dynamic-slice_fusion.3) | copy-start | bytes 245764 | tf_op jit(solution)/shard_map/while
  420.2 3.2 collective-permute-start
  423.3 76.0 %all-reduce.2.cloned.1.call-start = ((), (), s32[]{:S(2)}) async-start(), calls=%async_computation.10 | async-start | bytes 1310720 | tf_op jit(solution)/shard_map/while/body/eval_jaxpr/psum | solution.py:98
  439.0 6.9 copy-start
  445.8 3.6 copy-start.1
  484.6 16.2 %copy-start.3 = (bf16[1,64,640]{2,1,0:T(8,128)(2,1)S(1)}, bf16[1,64,640]{2,1,0:T(8,128)(2,1)}, u32[]{:S(2)}) copy-start(bf16[1,64,640]{2,1,0:T(8,128)(2,1)} %constant_dynamic-slice_fusion.3) | copy-start | bytes 245764 | tf_op jit(solution)/shard_map/while
  502.6 3.2 collective-permute-start
  505.8 75.9 %all-reduce.2.cloned.1.call-start = ((), (), s32[]{:S(2)}) async-start(), calls=%async_computation.10 | async-start | bytes 1310720 | tf_op jit(solution)/shard_map/while/body/eval_jaxpr/psum | solution.py:98
  521.3 6.9 copy-start
  528.2 3.6 copy-start.1
  566.9 16.2 %copy-start.3 = (bf16[1,64,640]{2,1,0:T(8,128)(2,1)S(1)}, bf16[1,64,640]{2,1,0:T(8,128)(2,1)}, u32[]{:S(2)}) copy-start(bf16[1,64,640]{2,1,0:T(8,128)(2,1)} %constant_dynamic-slice_fusion.3) | copy-start | bytes 245764 | tf_op jit(solution)/shard_map/while
  584.9 3.2 collective-permute-start
  588.1 75.9 %all-reduce.2.cloned.1.call-start = ((), (), s32[]{:S(2)}) async-start(), calls=%async_computation.10 | async-start | bytes 1310720 | tf_op jit(solution)/shard_map/while/body/eval_jaxpr/psum | solution.py:98
  603.6 6.9 copy-start
  610.5 3.6 copy-start.1
  649.3 16.2 %copy-start.3 = (bf16[1,64,640]{2,1,0:T(8,128)(2,1)S(1)}, bf16[1,64,640]{2,1,0:T(8,128)(2,1)}, u32[]{:S(2)}) copy-start(bf16[1,64,640]{2,1,0:T(8,128)(2,1)} %constant_dynamic-slice_fusion.3) | copy-start | bytes 245764 | tf_op jit(solution)/shard_map/while
  667.2 3.2 collective-permute-start
  670.4 75.9 %all-reduce.2.cloned.1.call-start = ((), (), s32[]{:S(2)}) async-start(), calls=%async_computation.10 | async-start | bytes 1310720 | tf_op jit(solution)/shard_map/while/body/eval_jaxpr/psum | solution.py:98
  685.9 6.9 copy-start
  692.8 3.6 copy-start.1
  731.6 16.2 %copy-start.3 = (bf16[1,64,640]{2,1,0:T(8,128)(2,1)S(1)}, bf16[1,64,640]{2,1,0:T(8,128)(2,1)}, u32[]{:S(2)}) copy-start(bf16[1,64,640]{2,1,0:T(8,128)(2,1)} %constant_dynamic-slice_fusion.3) | copy-start | bytes 245764 | tf_op jit(solution)/shard_map/while
  749.6 3.2 collective-permute-start
  752.7 76.3 %all-reduce.2.cloned.1.call-start = ((), (), s32[]{:S(2)}) async-start(), calls=%async_computation.10 | async-start | bytes 1310720 | tf_op jit(solution)/shard_map/while/body/eval_jaxpr/psum | solution.py:98
  768.7 6.9 copy-start
  775.5 3.6 copy-start.1
  814.3 16.2 %copy-start.3 = (bf16[1,64,640]{2,1,0:T(8,128)(2,1)S(1)}, bf16[1,64,640]{2,1,0:T(8,128)(2,1)}, u32[]{:S(2)}) copy-start(bf16[1,64,640]{2,1,0:T(8,128)(2,1)} %constant_dynamic-slice_fusion.3) | copy-start | bytes 245764 | tf_op jit(solution)/shard_map/while
  832.3 3.2 collective-permute-start
  835.5 76.6 %all-reduce.2.cloned.1.call-start = ((), (), s32[]{:S(2)}) async-start(), calls=%async_computation.10 | async-start | bytes 1310720 | tf_op jit(solution)/shard_map/while/body/eval_jaxpr/psum | solution.py:98
  851.7 6.9 copy-start
  858.6 3.6 copy-start.1
  897.4 16.2 %copy-start.3 = (bf16[1,64,640]{2,1,0:T(8,128)(2,1)S(1)}, bf16[1,64,640]{2,1,0:T(8,128)(2,1)}, u32[]{:S(2)}) copy-start(bf16[1,64,640]{2,1,0:T(8,128)(2,1)} %constant_dynamic-slice_fusion.3) | copy-start | bytes 245764 | tf_op jit(solution)/shard_map/while
  915.3 3.2 collective-permute-start
  918.5 76.6 %all-reduce.2.cloned.1.call-start = ((), (), s32[]{:S(2)}) async-start(), calls=%async_computation.10 | async-start | bytes 1310720 | tf_op jit(solution)/shard_map/while/body/eval_jaxpr/psum | solution.py:98
  934.8 6.9 copy-start
  941.6 3.6 copy-start.1
  980.4 16.2 %copy-start.3 = (bf16[1,64,640]{2,1,0:T(8,128)(2,1)S(1)}, bf16[1,64,640]{2,1,0:T(8,128)(2,1)}, u32[]{:S(2)}) copy-start(bf16[1,64,640]{2,1,0:T(8,128)(2,1)} %constant_dynamic-slice_fusion.3) | copy-start | bytes 245764 | tf_op jit(solution)/shard_map/while
  998.4 3.2 collective-permute-start
  1001.6 76.6 %all-reduce.2.cloned.1.call-start = ((), (), s32[]{:S(2)}) async-start(), calls=%async_computation.10 | async-start | bytes 1310720 | tf_op jit(solution)/shard_map/while/body/eval_jaxpr/psum | solution.py:98
  1017.8 6.9 copy-start
  1024.7 3.6 copy-start.1
  1063.5 16.2 %copy-start.3 = (bf16[1,64,640]{2,1,0:T(8,128)(2,1)S(1)}, bf16[1,64,640]{2,1,0:T(8,128)(2,1)}, u32[]{:S(2)}) copy-start(bf16[1,64,640]{2,1,0:T(8,128)(2,1)} %constant_dynamic-slice_fusion.3) | copy-start | bytes 245764 | tf_op jit(solution)/shard_map/while
  1081.4 3.2 collective-permute-start
  1084.6 166.6 %reduce-scatter.6.cloned.1.call-start = ((), (), s32[]{:S(2)}) async-start(), calls=%async_computation.4 | async-start | bytes 22118400 | tf_op jit(solution)/shard_map/reduce_scatter | solution.py:135
  1085.2 330.8 %reduce-scatter.8.cloned.1.call-start = ((), (), s32[]{:S(2)}) async-start(), calls=%async_computation.5 | async-start | bytes 22118400 | tf_op jit(solution)/shard_map/reduce_scatter | solution.py:136
  1085.8 494.9 %reduce-scatter.4.cloned.1.call-start = ((), (), s32[]{:S(2)}) async-start(), calls=%async_computation.3 | async-start | bytes 22118400 | tf_op jit(solution)/shard_map/reduce_scatter | solution.py:134
Sparse Core Ops, SparseCore 0:
  9.6 57.2 all-gather.12
  68.7 89.9 all-gather.16
  160.6 91.2 all-gather.18
  253.6 91.2 all-gather.14
  375.6 41.2 all-reduce.1
  453.3 39.9 all-reduce.1
  535.6 40.3 all-reduce.1
  617.9 40.7 all-reduce.1
  700.2 41.3 all-reduce.1
  783.0 41.4 all-reduce.1
  866.0 41.4 all-reduce.1
  949.1 41.4 all-reduce.1
  1032.1 41.5 all-reduce.1
  1088.8 162.2 reduce-scatter.5
  1254.7 161.1 reduce-scatter.7
  1419.5 161.1 reduce-scatter.3
